TPU v7x, 128 devices: a whole 4x4x4 slice. The times are simulated.
128 devices in a mesh: ia: 16 (over y, x), ja: 4 (over z_lo, core), col: 2 (over z_hi).
Axes of the slice: x: 4, y: 4, z: 4 (z_hi: 2, z_lo: 2; z = z_hi * 2 + z_lo), core: 2. Of those that a mesh axis runs over, the one named last changes fastest.
Arguments:
- pair_rep: bfloat16 [512, 512, 128], P('ia', 'ja'), may hold values from -6 to 6
- norm_gain: float32 [128], replicated, may hold values from 0.1 to 1.9
- weights: bfloat16 [4, 128, 128], P(None, None, 'col'), may hold values from -0.5 to 0.5
- residue_mask: int32 [512], replicated, may hold values 0 or 1
- product_grad: bfloat16 [512, 128, 512], P('ia', 'col', 'ja'), may hold values from -1 to 1
Outputs:
- pair_grad: bfloat16 [512, 512, 128], P('ia', 'ja')
- weight_grads: float32 [4, 128, 128], P(None, None, 'col')
All inputs are finite; a program needn't handle non-finite values.
Results may differ from a plain program's by a relative error of at most 0.0067.
Values may be sent and summed in bfloat16 or wider, within the bound.
No kernel may reach another device: no remote copies, remote signals or barrier semaphores. Data moves between devices by JAX's collectives and lax.ppermute only.
A program may use at most 128 MiB of HBM per device.

v0:
```python
import functools

import jax
import jax.numpy as jnp
from jax import lax
from jax.experimental import pallas as pl
from jax.experimental.pallas import tpu as pltpu
from jax.sharding import PartitionSpec as P

CLIP_LIMIT = 64.0
BF, F32 = jnp.bfloat16, jnp.float32


def normalised(x, gain=None):
    mean = jnp.mean(x, axis=-1, keepdims=True)
    centred = x - mean
    inv_std = lax.rsqrt(jnp.mean(centred * centred, axis=-1, keepdims=True) + 1e-05)
    return centred * inv_std, inv_std


def channels_first_kernel(x_ref, out_ref, flat):
    rows, chans, width = x_ref.shape
    flat[...] = x_ref[...].reshape(rows * chans, width).astype(F32)
    for c in range(chans):
        out_ref[c] = flat[pl.ds(c, rows, stride=chans), :].astype(BF)


def channels_first(x):
    rows, chans, width = x.shape
    return pl.pallas_call(
        channels_first_kernel,
        out_shape=jax.ShapeDtypeStruct((chans, rows, width), BF),
        scratch_shapes=[pltpu.VMEM((rows * chans, width), F32)],
        cost_estimate=pl.CostEstimate(flops=10**6, bytes_accessed=2 * x.size * 2, transcendentals=0),
        name="channels_first",
    )(x)


def project_kernel(x_ref, gain_ref, w_ref, valid_ref, sides_ref, factors_ref, normed_ref, flat):
    rows = x_ref.shape[0]
    groups, _, per, _, _ = sides_ref.shape
    half = groups * per
    gain = gain_ref[...]
    w = w_ref[...]

    def row(i, carry):
        unit, _ = normalised(x_ref[i].astype(F32))
        normed = (unit * gain).astype(BF)
        normed_ref[i] = normed
        proj = lax.dot_general(w, normed, (((1,), (1,)), ((), ())), preferred_element_type=F32)
        valid = valid_ref[pl.ds(i, 1), :]
        for side in range(2):
            at = 2 * side * half
            linear = proj[at : at + half]
            gate = jax.nn.sigmoid(proj[at + half : at + 2 * half])
            first = valid * gate
            both = first * linear
            flat[pl.ds(pl.multiple_of(i * 2 * half + side * half, half), half), :] = both
            factors_ref[i, at : at + half, :] = first
            factors_ref[i, at + half : at + 2 * half, :] = both * (1.0 - gate)
        return carry

    lax.fori_loop(0, rows, row, 0, unroll=2)
    for g in range(groups):
        for side in range(2):
            for c in range(per):
                first = side * half + g * per + c
                sides_ref[g, side, c] = flat[pl.ds(first, rows, stride=2 * half), :].astype(BF)


def project(x, gain, w, valid, groups, step):
    rows, cols, depth = x.shape
    half = w.shape[0] // 4
    per = half // groups
    return pl.pallas_call(
        project_kernel,
        grid=(rows // step,),
        in_specs=[
            pl.BlockSpec((step, cols, depth), lambda r: (r, 0, 0)),
            pl.BlockSpec((1, depth), lambda r: (0, 0)),
            pl.BlockSpec(w.shape, lambda r: (0, 0)),
            pl.BlockSpec((step, cols), lambda r: (r, 0)),
        ],
        out_specs=[
            pl.BlockSpec((groups, 2, per, step, cols), lambda r: (0, 0, 0, r, 0)),
            pl.BlockSpec((step, 4 * half, cols), lambda r: (r, 0, 0)),
            pl.BlockSpec((step, cols, depth), lambda r: (r, 0, 0)),
        ],
        out_shape=[
            jax.ShapeDtypeStruct((groups, 2, per, rows, cols), BF),
            jax.ShapeDtypeStruct((rows, 4 * half, cols), F32),
            jax.ShapeDtypeStruct((rows, cols, depth), BF),
        ],
        scratch_shapes=[pltpu.VMEM((step * 2 * half, cols), F32)],
        cost_estimate=pl.CostEstimate(flops=6 * 10**9, bytes_accessed=7 * 2**20, transcendentals=10**6),
        name="project",
    )(x, gain, w, valid)


def triangle_kernel(at_ref, sides_ref, *refs):
    *grads, out_ref = refs
    groups, _, _, rows, cols = sides_ref.shape
    share = groups // len(grads)
    left = sides_ref[:, 0, 0].reshape(groups * rows, cols)
    total = None
    for t, grad_ref in enumerate(grads):
        first = at_ref[t] * share
        grad = grad_ref[:, 0].reshape(groups * rows, cols)
        right = sides_ref[pl.ds(first, share), 1, 0].reshape(share * rows, cols)
        part = jnp.dot(grad, right, preferred_element_type=F32)
        total = part if total is None else total + part
        back = lax.dot_general(grad, left, (((0,), (0,)), ((), ())), preferred_element_type=F32)
        out_ref[pl.ds(first, share), 1, 0] = back.astype(BF).reshape(share, rows, cols)
    out_ref[:, 0, 0] = total.astype(BF).reshape(groups, rows, cols)


def triangle(at, sides, grads):
    groups, _, per, rows, cols = sides.shape
    side_spec = pl.BlockSpec((groups, 2, 1, rows, cols), lambda c, at: (0, 0, c, 0, 0))
    grad_spec = pl.BlockSpec((groups, 1, rows, cols), lambda c, at: (0, c, 0, 0))
    return pl.pallas_call(
        triangle_kernel,
        grid_spec=pltpu.PrefetchScalarGridSpec(
            num_scalar_prefetch=1,
            grid=(per,),
            in_specs=[side_spec] + [grad_spec] * len(grads),
            out_specs=side_spec,
        ),
        out_shape=jax.ShapeDtypeStruct(sides.shape, BF),
        cost_estimate=pl.CostEstimate(flops=4 * 10**9, bytes_accessed=5 * 2**20, transcendentals=0),
        name="triangle",
    )(at, sides, *grads)


def gate_kernel(in_ref, factors_ref, normed_ref, w_ref, out_ref, raw_ref, flat):
    groups, _, per, rows, _ = in_ref.shape
    half = groups * per
    for g in range(groups):
        for side in range(2):
            for c in range(per):
                first = (side * half + g * per + c) * rows
                flat[first : first + rows, :] = in_ref[g, side, c].astype(F32)

    @pl.when(pl.program_id(0) == 0)
    def _():
        raw_ref[...] = jnp.zeros_like(raw_ref)

    w = w_ref[...]

    def pair(i2, carry):
        made = []
        for e in range(2):
            i = i2 * 2 + e
            parts = []
            for side in range(2):
                incoming = flat[pl.ds(side * half * rows + i, half, stride=rows), :]
                at = 2 * side * half
                parts.append((incoming * factors_ref[i, at : at + half, :]).astype(BF))
                parts.append((incoming * factors_ref[i, at + half : at + 2 * half, :]).astype(BF))
            grads = jnp.concatenate(parts, axis=0)
            made.append(grads)
            back = lax.dot_general(grads, w, (((0,), (0,)), ((), ())), preferred_element_type=F32)
            out_ref[i] = back.astype(BF)
        both = jnp.concatenate(made, axis=1)
        cols, depth = normed_ref.shape[1:]
        normed = normed_ref[pl.ds(i2 * 2, 2)].reshape(2 * cols, depth)
        raw_ref[...] += jnp.dot(both, normed, preferred_element_type=F32)
        return carry

    lax.fori_loop(0, rows // 2, pair, 0)


def gate(incoming, factors, normed, w, step):
    groups, _, per, rows, cols = incoming.shape
    depth = normed.shape[-1]
    return pl.pallas_call(
        gate_kernel,
        grid=(rows // step,),
        in_specs=[
            pl.BlockSpec((groups, 2, per, step, cols), lambda r: (0, 0, 0, r, 0)),
            pl.BlockSpec((step,) + factors.shape[1:], lambda r: (r, 0, 0)),
            pl.BlockSpec((step, cols, depth), lambda r: (r, 0, 0)),
            pl.BlockSpec(w.shape, lambda r: (0, 0)),
        ],
        out_specs=[
            pl.BlockSpec((step, cols, depth), lambda r: (r, 0, 0)),
            pl.BlockSpec(w.shape, lambda r: (0, 0)),
        ],
        out_shape=[
            jax.ShapeDtypeStruct((rows, cols, depth), BF),
            jax.ShapeDtypeStruct(w.shape, F32),
        ],
        scratch_shapes=[pltpu.VMEM((2 * groups * per * step, cols), F32)],
        cost_estimate=pl.CostEstimate(flops=6 * 10**9, bytes_accessed=8 * 2**20, transcendentals=0),
        name="gate",
    )(incoming, factors, normed, w)


def finish_kernel(x_ref, gain_ref, own_ref, other_ref, out_ref):
    unit, inv_std = normalised(x_ref[...].astype(F32))
    scaled = (own_ref[...].astype(F32) + other_ref[...].astype(F32)) * gain_ref[...]
    mean = jnp.mean(scaled, axis=-1, keepdims=True)
    along = jnp.mean(scaled * unit, axis=-1, keepdims=True)
    out_ref[...] = (inv_std * (scaled - mean - unit * along)).astype(BF)


def finish(x, gain, own, other, step):
    rows, cols, depth = x.shape
    spec = pl.BlockSpec((step, cols, depth), lambda r: (r, 0, 0))
    return pl.pallas_call(
        finish_kernel,
        grid=(rows // step,),
        in_specs=[spec, pl.BlockSpec((1, 1, depth), lambda r: (0, 0, 0)), spec, spec],
        out_specs=spec,
        out_shape=jax.ShapeDtypeStruct(x.shape, BF),
        cost_estimate=pl.CostEstimate(flops=10**7, bytes_accessed=4 * 2**20, transcendentals=0),
        name="finish",
    )(x, gain.reshape(1, 1, depth), own, other)


def swapped(x, axis, bit):
    size = lax.axis_size(axis)
    return lax.ppermute(x, axis, [(i, i ^ bit) for i in range(size)])


def on_device(pair_rep, norm_gain, weights, residue_mask, product_grad):
    rows, cols, depth = pair_rep.shape
    chans = product_grad.shape[1]
    groups = lax.axis_size("ia")
    per = chans // groups
    here = lax.axis_index("ja")
    validity = residue_mask.astype(F32)
    row_valid = lax.dynamic_slice_in_dim(validity, lax.axis_index("ia") * rows, rows)
    col_valid = lax.dynamic_slice_in_dim(validity, here * cols, cols)
    pair_valid = row_valid[:, None] * col_valid[None, :]
    w = jnp.swapaxes(weights, 1, 2).reshape(4 * chans, depth)

    grads = channels_first(product_grad).reshape(groups, per, rows, cols)
    grads = lax.all_to_all(grads, "ia", 0, 0, tiled=True)
    far = swapped(grads, "ja", 2)
    sides, factors, normed = project(pair_rep, norm_gain[None], w, pair_valid, groups, 16)
    sides = lax.all_to_all(sides, "ia", 0, 0, tiled=True)
    near = swapped(grads, "ja", 1)
    farther = swapped(far, "ja", 1)
    at = jnp.stack([here, here ^ 1, here ^ 2, here ^ 3]).astype(jnp.int32)
    products = triangle(at, sides, (grads, near, far, farther))
    products = lax.all_to_all(products, "ia", 0, 0, tiled=True)
    own, raw = gate(products, factors, normed, w, 16)
    other = swapped(own, "col", 1)

    peers = ("ia", "ja")
    count = lax.axis_size(peers)
    pieces = lax.all_to_all(raw.reshape(count, -1, depth), peers, 0, 0, tiled=True)
    piece = jnp.sum(pieces, axis=0)
    whole = lax.all_to_all(jnp.broadcast_to(piece[None], pieces.shape), peers, 0, 0, tiled=True)
    whole = whole.reshape(4, chans, depth)
    squares = jnp.sum(whole * whole).reshape(1, 1)
    squares = squares + swapped(squares, "col", 1)
    factor = jnp.minimum(1.0, CLIP_LIMIT * lax.rsqrt(squares[0, 0] + 1e-06))
    weight_grads = jnp.swapaxes(whole, 1, 2) * factor
    pair_grad = finish(pair_rep, norm_gain, own, other, 8)
    return (pair_grad, weight_grads)


def solution(mesh):
    placed = (P("ia", "ja", None), P(), P(None, None, "col"), P(), P("ia", "col", "ja"))
    return jax.shard_map(
        on_device,
        mesh=mesh,
        in_specs=placed,
        out_specs=(P("ia", "ja", None), P(None, None, "col")),
        check_vma=False,
    )
```

profile of v0, /device:TPU:0, one launch (start us, length us, event | category | flops | bytes accessed | tf_op | source)
XLA Modules:
  0.0 140.0 jit_solution(4302575021434707203)
XLA Ops:
  0.6 2.5 %channels_first.1 = bf16[64,32,128]{2,1,0:T(8,128)(2,1)} custom-call(bf16[32,64,128]{2,1,0:T(8,128)(2,1)} %x_ref.4), custom_call_target="tpu_custom_call" | custom-call | flops 1000000 | bytes 1048576 | tf_op jit(solution)/shard_map/channels_first/pallas_call | solution.py:30
  3.1 7.1 %all-to-all-start.1 = ((bf16[16,4,32,128]{3,2,1,0:T(8,128)(2,1)}), bf16[16,4,32,128]{3,2,1,0:T(8,128)(2,1)S(1)}, u32[]{:S(2)}, u32[]{:S(2)}) async-start(bf16[16,4,32,128]{3,2,1,0:T(8,128)(2,1)} %bitcast.18), calls=%async_computation.1 | async-start | bytes 1048576 | tf_op jit(solution)/shard_map/all_to_all | solution.py:239
  10.3 0.7 convert_element_type.3
  11.1 0.7 broadcast_multiply_fusion.1.valid_ref
  11.8 10.0 %all-to-all-done.1.refs_0_ = bf16[16,4,32,128]{3,2,1,0:T(8,128)(2,1)S(1)} async-done(((bf16[16,4,32,128]{3,2,1,0:T(8,128)(2,1)}), bf16[16,4,32,128]{3,2,1,0:T(8,128)(2,1)S(1)}, u32[]{:S(2)}, u32[]{:S(2)}) %all-to-all-start.1) | async-done | bytes 524320 | tf_op jit(solution)/shard_map/all_to_all | solution.py:239
  21.8 1.9 %collective-permute-start.1 = (bf16[16,4,32,128]{3,2,1,0:T(8,128)(2,1)S(1)}, bf16[16,4,32,128]{3,2,1,0:T(8,128)(2,1)S(1)}, u32[]{:S(2)}, u32[]{:S(2)}) collective-permute-start(bf16[16,4,32,128]{3,2,1,0:T(8,128)(2,1)S(1)} %all-to-all-done.1.refs_0_), channel_id=1, source_target_pairs={{0,4},{2,6},{4,0},{6,2},{1,5},{3,7},{5,1},{7,3},{8,12},{10,14},{12... | collective-permute-start | bytes 1572872 | tf_op jit(solution)/shard_map/ppermute | solution.py:223
  23.7 10.0 %project.1 = (bf16[16,2,4,32,128]{4,3,2,1,0:T(8,128)(2,1)}, f32[32,256,128]{2,1,0:T(8,128)}, bf16[32,128,128]{2,1,0:T(8,128)(2,1)}) custom-call(bf16[32,128,128]{2,1,0:T(8,128)(2,1)} %x_ref.5, f32[1,128]{1,0:T(1,128)} %bitcast.22, bf16[256,128]{1,0:T(8,128)(2,1)} %bitcast.24, f32[32,128]{1,0:T(8,128)} %broadcast_multiply_fusion.1.valid_ref), custom_call_target="tpu_custom_call" | custom-call | flops 6000000000 | bytes 7340032 | tf_op jit(solution)/shard_map/project/pallas_call | solution.py:75
  33.7 3.7 %all-to-all-start = ((bf16[16,2,4,32,128]{4,3,2,1,0:T(8,128)(2,1)}), bf16[16,2,4,32,128]{4,3,2,1,0:T(8,128)(2,1)S(1)}, u32[]{:S(2)}, u32[]{:S(2)}) async-start(bf16[16,2,4,32,128]{4,3,2,1,0:T(8,128)(2,1)} %get-tuple-element.7), calls=%async_computation | async-start | bytes 2097152 | tf_op jit(solution)/shard_map/all_to_all | solution.py:242
  37.9 0.6 pad_add_fusion.at_ref
  38.5 14.9 %all-to-all-done.sides_ref = bf16[16,2,4,32,128]{4,3,2,1,0:T(8,128)(2,1)S(1)} async-done(((bf16[16,2,4,32,128]{4,3,2,1,0:T(8,128)(2,1)}), bf16[16,2,4,32,128]{4,3,2,1,0:T(8,128)(2,1)S(1)}, u32[]{:S(2)}, u32[]{:S(2)}) %all-to-all-start) | async-done | bytes 1048608 | tf_op jit(solution)/shard_map/all_to_all | solution.py:242
  53.5 0.9 copy-done.1
  54.6 0.8 copy-done.5
  55.4 5.4 %triangle.1 = bf16[16,2,4,32,128]{4,3,2,1,0:T(8,128)(2,1)} custom-call(s32[4]{0:T(128)} %pad_add_fusion.at_ref, bf16[16,2,4,32,128]{4,3,2,1,0:T(8,128)(2,1)} %copy-done.1, bf16[16,4,32,128]{3,2,1,0:T(8,128)(2,1)} %copy-done.2, bf16[16,4,32,128]{3,2,1,0:T(8,128)(2,1)} %copy-done.4, bf16[16,4,32,128]{3,2,1,0:T(8,128)(2,1)} %copy-done.3, ...), custom_call_target="tpu_custom_call" | custom-call | flops 4000000000 | bytes 5242880 | tf_op jit(solution)/shard_map/triangle/pallas_call | solution.py:121
  60.9 19.0 %all_to_all.25.in_ref = bf16[16,2,4,32,128]{4,3,2,1,0:T(8,128)(2,1)} all-to-all(bf16[16,2,4,32,128]{4,3,2,1,0:T(8,128)(2,1)} %triangle.1), channel_id=1, replica_groups=mesh['ia'=16,'ja'=4,'col'=2] {'ia'}, dimensions={0} | all-to-all | bytes 2097152 | tf_op jit(solution)/shard_map/all_to_all | solution.py:247
  79.9 7.7 %gate.1 = (bf16[32,128,128]{2,1,0:T(8,128)(2,1)}, f32[256,128]{1,0:T(8,128)}) custom-call(bf16[16,2,4,32,128]{4,3,2,1,0:T(8,128)(2,1)} %all_to_all.25.in_ref, f32[32,256,128]{2,1,0:T(8,128)} %get-tuple-element.8.factors_ref, bf16[32,128,128]{2,1,0:T(8,128)(2,1)} %get-tuple-element.9.normed_ref, bf16[256,128]{1,0:T(8,128)(2,1)} %bitcast.25), custom_call_target="tpu_custom_call" | custom-call | flops 6000000000 | bytes 8388608 | tf_op jit(solution)/shard_map/gate/pallas_call | solution.py:176
  87.6 3.6 %collective-permute-start.3 = (bf16[32,128,128]{2,1,0:T(8,128)(2,1)}, bf16[32,128,128]{2,1,0:T(8,128)(2,1)S(1)}, u32[]{:S(2)}, u32[]{:S(2)}) collective-permute-start(bf16[32,128,128]{2,1,0:T(8,128)(2,1)} %get-tuple-element.10.own_ref), channel_id=1, source_target_pairs={{0,1},{1,0},{2,3},{3,2},{4,5},{5,4},{6,7},{7,6},{8,9},{9,8},{10,11... | collective-permute-start | bytes 3145736 | tf_op jit(solution)/shard_map/ppermute | solution.py:223
  91.2 20.7 %all_to_all.26 = f32[64,4,128]{2,1,0:T(4,128)S(1)} all-to-all(f32[64,4,128]{2,1,0:T(4,128)} %bitcast.21), channel_id=1, replica_groups=mesh['ia'=16,'ja'=4,'col'=2] {'ia','ja'}, dimensions={0} | all-to-all | bytes 262144 | tf_op jit(solution)/shard_map/all_to_all | solution.py:253
  112.0 14.2 %all_to_all.27 = f32[64,4,128]{2,1,0:T(4,128)S(1)} all-to-all(f32[64,4,128]{2,1,0:T(4,128)S(1)} %broadcast_in_dim.5), channel_id=1, replica_groups=mesh['ia'=16,'ja'=4,'col'=2] {'ia','ja'}, dimensions={0} | all-to-all | bytes 262144 | tf_op jit(solution)/shard_map/all_to_all | solution.py:255
  126.2 0.7 multiply_reduce_fusion
  126.9 0.8 collective-permute-start.4
  127.7 4.3 %collective-permute-done.4 = f32[1,1]{1,0:T(1,128)} collective-permute-done((f32[1,1]{1,0:T(1,128)}, f32[1,1]{1,0:T(1,128)}, u32[]{:S(2)}, u32[]{:S(2)}) %collective-permute-start.4) | collective-permute-done | bytes 36 | tf_op jit(solution)/shard_map/ppermute | solution.py:223
  133.4 0.7 broadcast_multiply_fusion
  134.1 1.0 copy-done
  135.0 5.0 %finish.1 = bf16[32,128,128]{2,1,0:T(8,128)(2,1)} custom-call(bf16[32,128,128]{2,1,0:T(8,128)(2,1)} %x_ref.5, f32[1,1,128]{2,1,0:T(1,128)} %bitcast.23, bf16[32,128,128]{2,1,0:T(8,128)(2,1)} %get-tuple-element.10.own_ref, bf16[32,128,128]{2,1,0:T(8,128)(2,1)} %copy-done), custom_call_target="tpu_custom_call" | custom-call | flops 10000000 | bytes 4194304 | tf_op jit(solution)/shard_map/finish/pallas_call | solution.py:210
  (19 shorter events, 1.0 us)
Async XLA Ops:
  3.1 18.7 %all-to-all-start.1 = ((bf16[16,4,32,128]{3,2,1,0:T(8,128)(2,1)}), bf16[16,4,32,128]{3,2,1,0:T(8,128)(2,1)S(1)}, u32[]{:S(2)}, u32[]{:S(2)}) async-start(bf16[16,4,32,128]{3,2,1,0:T(8,128)(2,1)} %bitcast.18), calls=%async_computation.1 | async-start | bytes 1048576 | tf_op jit(solution)/shard_map/all_to_all | solution.py:239
  21.8 15.5 %copy-start.2 = (bf16[16,4,32,128]{3,2,1,0:T(8,128)(2,1)}, bf16[16,4,32,128]{3,2,1,0:T(8,128)(2,1)S(1)}, u32[]{:S(2)}) copy-start(bf16[16,4,32,128]{3,2,1,0:T(8,128)(2,1)S(1)} %all-to-all-done.1.refs_0_) | copy-start | bytes 1572868
  21.8 15.6 %collective-permute-start.1 = (bf16[16,4,32,128]{3,2,1,0:T(8,128)(2,1)S(1)}, bf16[16,4,32,128]{3,2,1,0:T(8,128)(2,1)S(1)}, u32[]{:S(2)}, u32[]{:S(2)}) collective-permute-start(bf16[16,4,32,128]{3,2,1,0:T(8,128)(2,1)S(1)} %all-to-all-done.1.refs_0_), channel_id=1, source_target_pairs={{0,4},{2,6},{4,0},{6,2},{1,5},{3,7},{5,1},{7,3},{8,12},{10,14},{12... | collective-permute-start | bytes 1572872 | tf_op jit(solution)/shard_map/ppermute | solution.py:223
  33.7 19.8 %all-to-all-start = ((bf16[16,2,4,32,128]{4,3,2,1,0:T(8,128)(2,1)}), bf16[16,2,4,32,128]{4,3,2,1,0:T(8,128)(2,1)S(1)}, u32[]{:S(2)}, u32[]{:S(2)}) async-start(bf16[16,2,4,32,128]{4,3,2,1,0:T(8,128)(2,1)} %get-tuple-element.7), calls=%async_computation | async-start | bytes 2097152 | tf_op jit(solution)/shard_map/all_to_all | solution.py:242
  37.3 16.1 %collective-permute-start = (bf16[16,4,32,128]{3,2,1,0:T(8,128)(2,1)S(1)}, bf16[16,4,32,128]{3,2,1,0:T(8,128)(2,1)S(1)}, u32[]{:S(2)}, u32[]{:S(2)}) collective-permute-start(bf16[16,4,32,128]{3,2,1,0:T(8,128)(2,1)S(1)} %all-to-all-done.1.refs_0_), channel_id=1, source_target_pairs={{0,2},{2,0},{4,6},{6,4},{1,3},{3,1},{5,7},{7,5},{8,10},{10,8},{12,... | collective-permute-start | bytes 1572872 | tf_op jit(solution)/shard_map/ppermute | solution.py:223
  37.5 16.0 %copy-start.3 = (bf16[16,4,32,128]{3,2,1,0:T(8,128)(2,1)}, bf16[16,4,32,128]{3,2,1,0:T(8,128)(2,1)S(1)}, u32[]{:S(2)}) copy-start(bf16[16,4,32,128]{3,2,1,0:T(8,128)(2,1)S(1)} %collective-permute-done.1.refs_2_) | copy-start | bytes 1572868
  37.5 16.0 %collective-permute-start.2 = (bf16[16,4,32,128]{3,2,1,0:T(8,128)(2,1)S(1)}, bf16[16,4,32,128]{3,2,1,0:T(8,128)(2,1)S(1)}, u32[]{:S(2)}, u32[]{:S(2)}) collective-permute-start(bf16[16,4,32,128]{3,2,1,0:T(8,128)(2,1)S(1)} %collective-permute-done.1.refs_2_), channel_id=1, source_target_pairs={{0,2},{2,0},{4,6},{6,4},{1,3},{3,1},{5,7},{7,5},{8,10},{10,8},{12,... | collective-permute-start | bytes 1572872 | tf_op jit(solution)/shard_map/ppermute | solution.py:223
  53.5 1.0 copy-start.1
  53.5 1.1 copy-start.4
  54.6 0.8 copy-start.5
  87.6 46.4 %collective-permute-start.3 = (bf16[32,128,128]{2,1,0:T(8,128)(2,1)}, bf16[32,128,128]{2,1,0:T(8,128)(2,1)S(1)}, u32[]{:S(2)}, u32[]{:S(2)}) collective-permute-start(bf16[32,128,128]{2,1,0:T(8,128)(2,1)} %get-tuple-element.10.own_ref), channel_id=1, source_target_pairs={{0,1},{1,0},{2,3},{3,2},{4,5},{5,4},{6,7},{7,6},{8,9},{9,8},{10,11... | collective-permute-start | bytes 3145736 | tf_op jit(solution)/shard_map/ppermute | solution.py:223
  126.9 5.2 %collective-permute-start.4 = (f32[1,1]{1,0:T(1,128)}, f32[1,1]{1,0:T(1,128)}, u32[]{:S(2)}, u32[]{:S(2)}) collective-permute-start(f32[1,1]{1,0:T(1,128)} %bitcast.10), channel_id=1, source_target_pairs={{0,1},{1,0},{2,3},{3,2},{4,5},{5,4},{6,7},{7,6},{8,9},{9,8},{10,11... | collective-permute-start | bytes 20 | tf_op jit(solution)/shard_map/ppermute | solution.py:223
  134.1 1.0 copy-start
where the time goes:
time: 141 us; the launch traced here: 140 us
  blocking collectives  54 us (38%)
  Pallas kernels  30.6 us (22%)
  waiting for transfers between devices  29.3 us (21%)
  starting transfers between devices  17.7 us (13%)
  other arithmetic  3.37 us (2%)
  local copies, waits for them, and re-layouts  3.12 us (2%)
  between operations  2.03 us (1%)
    all_to_all x1, blocking collectives, on_device(): lax.all_to_all(raw.reshape(count, -1, depth), peers, 0, 0, tiled=True)  20.7 us
    all_to_all x1, blocking collectives, on_device(): products = lax.all_to_all(products, 'ia', 0, 0, tiled=True)  19 us
    all_to_all x1, waiting for transfers between devices, on_device(): sides = lax.all_to_all(sides, 'ia', 0, 0, tiled=True)  14.9 us
    all_to_all x1, blocking collectives, on_device(): lax.all_to_all(jnp.broadcast_to(piece[None], pieces.shape), peers, 0, 0,...  14.2 us
    all_to_all x1, waiting for transfers between devices, on_device(): grads = lax.all_to_all(grads, 'ia', 0, 0, tiled=True)  10 us
    pallas_call x1, Pallas kernels, project(): pl.pallas_call(project_kernel, grid=(rows // step,), in_specs=[pl.BlockSp...  9.96 us
    pallas_call x1, Pallas kernels, gate(): pl.pallas_call(gate_kernel, grid=(rows // step,), in_specs=[pl.BlockSpec(...  7.72 us
    all_to_all x1, starting transfers between devices, on_device(): grads = lax.all_to_all(grads, 'ia', 0, 0, tiled=True)  7.15 us
  transfers between devices with their start and end apart: 7, of which 3 were waited for; matrix products, arithmetic and copies ran while one was open for 3% of the time, Pallas kernels for 7%

commit v1 on v0

--- a/solution.py
+++ b/solution.py
@@ -1,5 +1,3 @@
-import functools
-
 import jax
 import jax.numpy as jnp
 from jax import lax
@@ -7,11 +5,12 @@
 from jax.experimental.pallas import tpu as pltpu
 from jax.sharding import PartitionSpec as P
 
+
 CLIP_LIMIT = 64.0
 BF, F32 = jnp.bfloat16, jnp.float32
 
 
-def normalised(x, gain=None):
+def normalised(x):
     mean = jnp.mean(x, axis=-1, keepdims=True)
     centred = x - mean
     inv_std = lax.rsqrt(jnp.mean(centred * centred, axis=-1, keepdims=True) + 1e-05)
@@ -237,8 +236,9 @@
 
     grads = channels_first(product_grad).reshape(groups, per, rows, cols)
     grads = lax.all_to_all(grads, "ia", 0, 0, tiled=True)
+    sides, factors, normed = project(pair_rep, norm_gain[None], w, pair_valid, groups, 16)
+    grads, sides = lax.optimization_barrier((grads, sides))
     far = swapped(grads, "ja", 2)
-    sides, factors, normed = project(pair_rep, norm_gain[None], w, pair_valid, groups, 16)
     sides = lax.all_to_all(sides, "ia", 0, 0, tiled=True)
     near = swapped(grads, "ja", 1)
     farther = swapped(far, "ja", 1)
@@ -246,13 +246,12 @@
     products = triangle(at, sides, (grads, near, far, farther))
     products = lax.all_to_all(products, "ia", 0, 0, tiled=True)
     own, raw = gate(products, factors, normed, w, 16)
+    raw = raw + swapped(raw, "ja", 2)
     other = swapped(own, "col", 1)
-
-    peers = ("ia", "ja")
-    count = lax.axis_size(peers)
-    pieces = lax.all_to_all(raw.reshape(count, -1, depth), peers, 0, 0, tiled=True)
+    raw = raw + swapped(raw, "ja", 1)
+    pieces = lax.all_to_all(raw.reshape(groups, -1, depth), "ia", 0, 0, tiled=True)
     piece = jnp.sum(pieces, axis=0)
-    whole = lax.all_to_all(jnp.broadcast_to(piece[None], pieces.shape), peers, 0, 0, tiled=True)
+    whole = lax.all_to_all(jnp.broadcast_to(piece[None], pieces.shape), "ia", 0, 0, tiled=True)
     whole = whole.reshape(4, chans, depth)
     squares = jnp.sum(whole * whole).reshape(1, 1)
     squares = squares + swapped(squares, "col", 1)

time: 141 us -> 149 us (1.057)
  waiting for transfers between devices: 29.3 us -> 44.9 us
  blocking collectives: 54 us -> 42.2 us
  starting transfers between devices: 17.7 us -> 21 us
    ppermute x5 -> x7, waiting for transfers between devices: 4.33 us -> 33.5 us  [swapped(): return lax.ppermute(x, axis, [(i, i ^ bit) for i in range(size)])]
    all_to_all x2, blocking collectives: 34.9 us -> 21.6 us  [the longest x1 11.1 us: on_device(): lax.all_to_all(jnp.broadcast_to(piece[None], pieces.shape), 'ia', 0, 0, t...]
    all_to_all x1, waiting for transfers between devices: 10 us -> 0.05 us  [on_device(): grads = lax.all_to_all(grads, 'ia', 0, 0, tiled=True)]
    all_to_all x1, waiting for transfers between devices: 14.9 us -> 11.4 us  [on_device(): sides = lax.all_to_all(sides, 'ia', 0, 0, tiled=True)]
    all_to_all x1, starting transfers between devices: 3.66 us -> 7.21 us  [on_device(): sides = lax.all_to_all(sides, 'ia', 0, 0, tiled=True)]
    all_to_all x1, blocking collectives: 19 us -> 20.5 us  [on_device(): products = lax.all_to_all(products, 'ia', 0, 0, tiled=True)]
    ppermute x5 -> x7, starting transfers between devices: 6.9 us -> 6.61 us  [swapped(): return lax.ppermute(x, axis, [(i, i ^ bit) for i in range(size)])]
  transfers between devices with their start and end apart: 7 -> 9, of which waited for: 3 -> 5; matrix products, arithmetic and copies ran while one was open for 3% -> 3% of each run, Pallas kernels for 7% -> 7%
where the time goes in v1:
time: 149 us; the launch traced here: 148 us
  waiting for transfers between devices  44.9 us (30%)
  blocking collectives  42.2 us (28%)
  Pallas kernels  30.6 us (21%)
  starting transfers between devices  21 us (14%)
  other arithmetic  4.39 us (3%)
  local copies, waits for them, and re-layouts  2.91 us (2%)
  between operations  1.98 us (1%)
    ppermute x7, waiting for transfers between devices, swapped(): return lax.ppermute(x, axis, [(i, i ^ bit) for i in range(size)])  33.5 us
    all_to_all x1, blocking collectives, on_device(): products = lax.all_to_all(products, 'ia', 0, 0, tiled=True)  20.5 us
    all_to_all x1, waiting for transfers between devices, on_device(): sides = lax.all_to_all(sides, 'ia', 0, 0, tiled=True)  11.4 us
    all_to_all x1, blocking collectives, on_device(): lax.all_to_all(jnp.broadcast_to(piece[None], pieces.shape), 'ia', 0, 0, t...  11.1 us
    all_to_all x1, blocking collectives, on_device(): lax.all_to_all(raw.reshape(groups, -1, depth), 'ia', 0, 0, tiled=True)  10.6 us
    pallas_call x1, Pallas kernels, project(): pl.pallas_call(project_kernel, grid=(rows // step,), in_specs=[pl.BlockSp...  9.96 us
    pallas_call x1, Pallas kernels, gate(): pl.pallas_call(gate_kernel, grid=(rows // step,), in_specs=[pl.BlockSpec(...  7.7 us
    all_to_all x1, starting transfers between devices, on_device(): sides = lax.all_to_all(sides, 'ia', 0, 0, tiled=True)  7.21 us
  transfers between devices with their start and end apart: 9, of which 5 were waited for; matrix products, arithmetic and copies ran while one was open for 3% of the time, Pallas kernels for 7%

profile of v1, /device:TPU:0, one launch (start us, length us, event | category | flops | bytes accessed | tf_op | source)
XLA Modules:
  0.0 147.9 jit_solution(1499988217889260195)
XLA Ops:
  0.6 2.5 %channels_first.1 = bf16[64,32,128]{2,1,0:T(8,128)(2,1)} custom-call(bf16[32,64,128]{2,1,0:T(8,128)(2,1)} %x_ref.3), custom_call_target="tpu_custom_call" | custom-call | flops 1000000 | bytes 1048576 | tf_op jit(solution)/shard_map/channels_first/pallas_call | solution.py:29
  3.2 7.1 %all-to-all-start = ((bf16[16,4,32,128]{3,2,1,0:T(8,128)(2,1)}), bf16[16,4,32,128]{3,2,1,0:T(8,128)(2,1)S(1)}, u32[]{:S(2)}, u32[]{:S(2)}) async-start(bf16[16,4,32,128]{3,2,1,0:T(8,128)(2,1)} %bitcast.16), calls=%async_computation | async-start | bytes 1048576 | tf_op jit(solution)/shard_map/all_to_all | solution.py:238
  10.3 0.7 convert_element_type.3
  11.8 10.0 %project.1 = (bf16[16,2,4,32,128]{4,3,2,1,0:T(8,128)(2,1)}, f32[32,256,128]{2,1,0:T(8,128)}, bf16[32,128,128]{2,1,0:T(8,128)(2,1)}) custom-call(bf16[32,128,128]{2,1,0:T(8,128)(2,1)} %x_ref.5, f32[1,128]{1,0:T(1,128)} %bitcast.19, bf16[256,128]{1,0:T(8,128)(2,1)} %bitcast.21, f32[32,128]{1,0:T(8,128)} %broadcast_multiply_fusion.1.valid_ref), custom_call_target="tpu_custom_call" | custom-call | flops 6000000000 | bytes 7340032 | tf_op jit(solution)/shard_map/project/pallas_call | solution.py:74
  21.8 2.0 %collective-permute-start.1 = (bf16[16,4,32,128]{3,2,1,0:T(8,128)(2,1)S(1)}, bf16[16,4,32,128]{3,2,1,0:T(8,128)(2,1)S(1)}, u32[]{:S(2)}, u32[]{:S(2)}) collective-permute-start(bf16[16,4,32,128]{3,2,1,0:T(8,128)(2,1)S(1)} %all-to-all-done.refs_0_), channel_id=1, source_target_pairs={{0,4},{2,6},{4,0},{6,2},{1,5},{3,7},{5,1},{7,3},{8,12},{10,14},{12... | collective-permute-start | bytes 1572872 | tf_op jit(solution)/shard_map/ppermute | solution.py:222
  23.8 7.2 %all-to-all-start.1 = ((bf16[16,2,4,32,128]{4,3,2,1,0:T(8,128)(2,1)}), bf16[16,2,4,32,128]{4,3,2,1,0:T(8,128)(2,1)S(1)}, u32[]{:S(2)}, u32[]{:S(2)}) async-start(bf16[16,2,4,32,128]{4,3,2,1,0:T(8,128)(2,1)} %get-tuple-element.10), calls=%async_computation.1 | async-start | bytes 2097152 | tf_op jit(solution)/shard_map/all_to_all | solution.py:242
  31.1 4.3 %collective-permute-done.1.refs_2_ = bf16[16,4,32,128]{3,2,1,0:T(8,128)(2,1)S(1)} collective-permute-done((bf16[16,4,32,128]{3,2,1,0:T(8,128)(2,1)S(1)}, bf16[16,4,32,128]{3,2,1,0:T(8,128)(2,1)S(1)}, u32[]{:S(2)}, u32[]{:S(2)}) %collective-permute-start.1) | collective-permute-done | bytes 524320 | tf_op jit(solution)/shard_map/ppermute | solution.py:222
  35.4 0.8 pad_add_fusion.at_ref
  36.2 11.4 %all-to-all-done.1.sides_ref = bf16[16,2,4,32,128]{4,3,2,1,0:T(8,128)(2,1)S(1)} async-done(((bf16[16,2,4,32,128]{4,3,2,1,0:T(8,128)(2,1)}), bf16[16,2,4,32,128]{4,3,2,1,0:T(8,128)(2,1)S(1)}, u32[]{:S(2)}, u32[]{:S(2)}) %all-to-all-start.1) | async-done | bytes 1048608 | tf_op jit(solution)/shard_map/all_to_all | solution.py:242
  47.6 0.9 copy-done.1
  48.5 0.8 copy-done.5
  49.4 5.4 %triangle.1 = bf16[16,2,4,32,128]{4,3,2,1,0:T(8,128)(2,1)} custom-call(s32[4]{0:T(128)} %pad_add_fusion.at_ref, bf16[16,2,4,32,128]{4,3,2,1,0:T(8,128)(2,1)} %copy-done.1, bf16[16,4,32,128]{3,2,1,0:T(8,128)(2,1)} %copy-done.2, bf16[16,4,32,128]{3,2,1,0:T(8,128)(2,1)} %copy-done.4, bf16[16,4,32,128]{3,2,1,0:T(8,128)(2,1)} %copy-done.3, ...), custom_call_target="tpu_custom_call" | custom-call | flops 4000000000 | bytes 5242880 | tf_op jit(solution)/shard_map/triangle/pallas_call | solution.py:120
  54.8 20.5 %all_to_all.25.in_ref = bf16[16,2,4,32,128]{4,3,2,1,0:T(8,128)(2,1)} all-to-all(bf16[16,2,4,32,128]{4,3,2,1,0:T(8,128)(2,1)} %triangle.1), channel_id=1, replica_groups=mesh['ia'=16,'ja'=4,'col'=2] {'ia'}, dimensions={0} | all-to-all | bytes 2097152 | tf_op jit(solution)/shard_map/all_to_all | solution.py:247
  75.4 7.7 %gate.1 = (bf16[32,128,128]{2,1,0:T(8,128)(2,1)}, f32[256,128]{1,0:T(8,128)}) custom-call(bf16[16,2,4,32,128]{4,3,2,1,0:T(8,128)(2,1)} %all_to_all.25.in_ref, f32[32,256,128]{2,1,0:T(8,128)} %get-tuple-element.12.factors_ref, bf16[32,128,128]{2,1,0:T(8,128)(2,1)} %get-tuple-element.13.normed_ref, bf16[256,128]{1,0:T(8,128)(2,1)} %bitcast.22), custom_call_target="tpu_custom_call" | custom-call | flops 6000000000 | bytes 8388608 | tf_op jit(solution)/shard_map/gate/pallas_call | solution.py:175
  83.1 3.6 %collective-permute-start.3 = (bf16[32,128,128]{2,1,0:T(8,128)(2,1)}, bf16[32,128,128]{2,1,0:T(8,128)(2,1)S(1)}, u32[]{:S(2)}, u32[]{:S(2)}) collective-permute-start(bf16[32,128,128]{2,1,0:T(8,128)(2,1)} %get-tuple-element.14.own_ref), channel_id=1, source_target_pairs={{0,1},{1,0},{2,3},{3,2},{4,5},{5,4},{6,7},{7,6},{8,9},{9,8},{10,11... | collective-permute-start | bytes 3145736 | tf_op jit(solution)/shard_map/ppermute | solution.py:222
  86.6 23.4 %collective-permute-done.4 = f32[256,128]{1,0:T(8,128)S(1)} collective-permute-done((f32[256,128]{1,0:T(8,128)}, f32[256,128]{1,0:T(8,128)S(1)}, u32[]{:S(2)}, u32[]{:S(2)}) %collective-permute-start.4) | collective-permute-done | bytes 131104 | tf_op jit(solution)/shard_map/ppermute | solution.py:222
  110.0 0.9 add.21
  111.1 1.3 collective-permute-done.5
  112.4 10.6 %all_to_all.26 = f32[16,16,128]{2,1,0:T(8,128)S(1)} all-to-all(f32[16,16,128]{2,1,0:T(8,128)S(1)} %bitcast.17), channel_id=1, replica_groups=mesh['ia'=16,'ja'=4,'col'=2] {'ia'}, dimensions={0} | all-to-all | bytes 262144 | tf_op jit(solution)/shard_map/all_to_all | solution.py:252
  123.0 11.1 %all_to_all.27 = f32[16,16,128]{2,1,0:T(8,128)S(1)} all-to-all(f32[16,16,128]{2,1,0:T(8,128)S(1)} %broadcast_in_dim.5), channel_id=1, replica_groups=mesh['ia'=16,'ja'=4,'col'=2] {'ia'}, dimensions={0} | all-to-all | bytes 262144 | tf_op jit(solution)/shard_map/all_to_all | solution.py:254
  134.7 0.9 collective-permute-start.6
  135.6 4.4 %collective-permute-done.6 = f32[1,1]{1,0:T(1,128)} collective-permute-done((f32[1,1]{1,0:T(1,128)}, f32[1,1]{1,0:T(1,128)}, u32[]{:S(2)}, u32[]{:S(2)}) %collective-permute-start.6) | collective-permute-done | bytes 36 | tf_op jit(solution)/shard_map/ppermute | solution.py:222
  142.0 1.0 copy-done
  142.9 5.0 %finish.1 = bf16[32,128,128]{2,1,0:T(8,128)(2,1)} custom-call(bf16[32,128,128]{2,1,0:T(8,128)(2,1)} %x_ref.5, f32[1,1,128]{2,1,0:T(1,128)} %bitcast.20, bf16[32,128,128]{2,1,0:T(8,128)(2,1)} %get-tuple-element.14.own_ref, bf16[32,128,128]{2,1,0:T(8,128)(2,1)} %copy-done), custom_call_target="tpu_custom_call" | custom-call | flops 10000000 | bytes 4194304 | tf_op jit(solution)/shard_map/finish/pallas_call | solution.py:209
  (25 shorter events, 2.4 us)
Async XLA Ops:
  3.2 18.7 %all-to-all-start = ((bf16[16,4,32,128]{3,2,1,0:T(8,128)(2,1)}), bf16[16,4,32,128]{3,2,1,0:T(8,128)(2,1)S(1)}, u32[]{:S(2)}, u32[]{:S(2)}) async-start(bf16[16,4,32,128]{3,2,1,0:T(8,128)(2,1)} %bitcast.16), calls=%async_computation | async-start | bytes 1048576 | tf_op jit(solution)/shard_map/all_to_all | solution.py:238
  21.8 25.7 %copy-start.2 = (bf16[16,4,32,128]{3,2,1,0:T(8,128)(2,1)}, bf16[16,4,32,128]{3,2,1,0:T(8,128)(2,1)S(1)}, u32[]{:S(2)}) copy-start(bf16[16,4,32,128]{3,2,1,0:T(8,128)(2,1)S(1)} %all-to-all-done.refs_0_) | copy-start | bytes 1572868
  21.8 13.6 %collective-permute-start.1 = (bf16[16,4,32,128]{3,2,1,0:T(8,128)(2,1)S(1)}, bf16[16,4,32,128]{3,2,1,0:T(8,128)(2,1)S(1)}, u32[]{:S(2)}, u32[]{:S(2)}) collective-permute-start(bf16[16,4,32,128]{3,2,1,0:T(8,128)(2,1)S(1)} %all-to-all-done.refs_0_), channel_id=1, source_target_pairs={{0,4},{2,6},{4,0},{6,2},{1,5},{3,7},{5,1},{7,3},{8,12},{10,14},{12... | collective-permute-start | bytes 1572872 | tf_op jit(solution)/shard_map/ppermute | solution.py:222
  23.8 23.8 %all-to-all-start.1 = ((bf16[16,2,4,32,128]{4,3,2,1,0:T(8,128)(2,1)}), bf16[16,2,4,32,128]{4,3,2,1,0:T(8,128)(2,1)S(1)}, u32[]{:S(2)}, u32[]{:S(2)}) async-start(bf16[16,2,4,32,128]{4,3,2,1,0:T(8,128)(2,1)} %get-tuple-element.10), calls=%async_computation.1 | async-start | bytes 2097152 | tf_op jit(solution)/shard_map/all_to_all | solution.py:242
  31.0 5.2 %collective-permute-start = (bf16[16,4,32,128]{3,2,1,0:T(8,128)(2,1)S(1)}, bf16[16,4,32,128]{3,2,1,0:T(8,128)(2,1)S(1)}, u32[]{:S(2)}, u32[]{:S(2)}) collective-permute-start(bf16[16,4,32,128]{3,2,1,0:T(8,128)(2,1)S(1)} %all-to-all-done.refs_0_), channel_id=1, source_target_pairs={{0,2},{2,0},{4,6},{6,4},{1,3},{3,1},{5,7},{7,5},{8,10},{10,8},{12,... | collective-permute-start | bytes 1572872 | tf_op jit(solution)/shard_map/ppermute | solution.py:222
  35.4 12.1 %copy-start.3 = (bf16[16,4,32,128]{3,2,1,0:T(8,128)(2,1)}, bf16[16,4,32,128]{3,2,1,0:T(8,128)(2,1)S(1)}, u32[]{:S(2)}) copy-start(bf16[16,4,32,128]{3,2,1,0:T(8,128)(2,1)S(1)} %collective-permute-done.1.refs_2_) | copy-start | bytes 1572868
  35.4 12.1 %collective-permute-start.2 = (bf16[16,4,32,128]{3,2,1,0:T(8,128)(2,1)S(1)}, bf16[16,4,32,128]{3,2,1,0:T(8,128)(2,1)S(1)}, u32[]{:S(2)}, u32[]{:S(2)}) collective-permute-start(bf16[16,4,32,128]{3,2,1,0:T(8,128)(2,1)S(1)} %collective-permute-done.1.refs_2_), channel_id=1, source_target_pairs={{0,2},{2,0},{4,6},{6,4},{1,3},{3,1},{5,7},{7,5},{8,10},{10,8},{12,... | collective-permute-start | bytes 1572872 | tf_op jit(solution)/shard_map/ppermute | solution.py:222
  36.2 11.4 %copy-start.4 = (bf16[16,4,32,128]{3,2,1,0:T(8,128)(2,1)}, bf16[16,4,32,128]{3,2,1,0:T(8,128)(2,1)S(1)}, u32[]{:S(2)}) copy-start(bf16[16,4,32,128]{3,2,1,0:T(8,128)(2,1)S(1)} %collective-permute-done.refs_1_) | copy-start | bytes 1572868
  47.6 1.0 copy-start.1
  48.5 0.8 copy-start.5
  83.1 58.9 %collective-permute-start.3 = (bf16[32,128,128]{2,1,0:T(8,128)(2,1)}, bf16[32,128,128]{2,1,0:T(8,128)(2,1)S(1)}, u32[]{:S(2)}, u32[]{:S(2)}) collective-permute-start(bf16[32,128,128]{2,1,0:T(8,128)(2,1)} %get-tuple-element.14.own_ref), channel_id=1, source_target_pairs={{0,1},{1,0},{2,3},{3,2},{4,5},{5,4},{6,7},{7,6},{8,9},{9,8},{10,11... | collective-permute-start | bytes 3145736 | tf_op jit(solution)/shard_map/ppermute | solution.py:222
  86.6 23.4 %collective-permute-start.4 = (f32[256,128]{1,0:T(8,128)}, f32[256,128]{1,0:T(8,128)S(1)}, u32[]{:S(2)}, u32[]{:S(2)}) collective-permute-start(f32[256,128]{1,0:T(8,128)} %get-tuple-element.15), channel_id=1, source_target_pairs={{0,4},{2,6},{4,0},{6,2},{1,5},{3,7},{5,1},{7,3},{8,12},{10,14},{12... | collective-permute-start | bytes 393224 | tf_op jit(solution)/shard_map/ppermute | solution.py:222
  111.0 1.4 collective-permute-start.5
  134.7 5.3 %collective-permute-start.6 = (f32[1,1]{1,0:T(1,128)}, f32[1,1]{1,0:T(1,128)}, u32[]{:S(2)}, u32[]{:S(2)}) collective-permute-start(f32[1,1]{1,0:T(1,128)} %bitcast.10), channel_id=1, source_target_pairs={{0,1},{1,0},{2,3},{3,2},{4,5},{5,4},{6,7},{7,6},{8,9},{9,8},{10,11... | collective-permute-start | bytes 20 | tf_op jit(solution)/shard_map/ppermute | solution.py:222
  142.0 1.0 copy-start
